TPU v7x, 256 devices: a whole 4x4x8 slice. The times are simulated.
256 devices in a mesh: section: 2 (over core), row: 16 (over y, x), col: 8 (over z).
Axes of the slice: x: 4, y: 4, z: 8, core: 2. Of those that a mesh axis runs over, the one named last changes fastest.
Arguments:
- section_inputs: bfloat16 [2, 2, 192, 4096], P('section', None, 'col', 'row'), may hold values from -6 to 6
- out_grad: bfloat16 [2, 192, 4096], P(None, 'col', 'row'), may hold values from -6 to 6
- gate_weight: bfloat16 [2, 4096, 14336], P('section', 'row', 'col'), may hold values from -0.09375 to 0.09375
- up_weight: bfloat16 [2, 4096, 14336], P('section', 'row', 'col'), may hold values from -0.09375 to 0.09375
- down_weight: bfloat16 [2, 14336, 4096], P('section', 'col', 'row'), may hold values from -0.046875 to 0.046875
Outputs:
- input_grads: bfloat16 [2, 2, 192, 4096], P('section', None, 'col', 'row')
- grad_gate: float32 [2, 4096, 14336], P('section', 'row', 'col')
- grad_up: float32 [2, 4096, 14336], P('section', 'row', 'col')
- grad_down: float32 [2, 14336, 4096], P('section', 'col', 'row')
All inputs are finite; a program needn't handle non-finite values.
Results may differ from a plain program's by a relative error of at most 0.025.
Values may be sent and summed in bfloat16 or wider, within the bound.
A program may use at most 64 MiB of HBM per device.

v0:
```python
import jax
import jax.numpy as jnp
from jax import lax
from jax.sharding import PartitionSpec as P

CONTRACT_ROWS = (((0,), (0,)), ((), ()))
CONTRACT_COLS = (((1,), (1,)), ((), ()))


def cut_along(value, dim, count):
    before, after = (value.shape[:dim], value.shape[dim + 1 :])
    return jnp.moveaxis(value.reshape(*before, count, -1, *after), dim, 0)


def summed_on_arrival(value, axis, dim):
    count = lax.axis_size(axis)
    pieces = lax.all_to_all(cut_along(value, dim, count), axis, 0, 0, tiled=True)
    return jnp.sum(pieces.astype(jnp.float32), axis=0)


def in_order(pieces, dim):
    dims = list(pieces.shape[1:])
    dims[dim] *= pieces.shape[0]
    return jnp.moveaxis(pieces, 0, dim).reshape(dims)


def from_everyone(value, axis):
    count = lax.axis_size(axis)
    return lax.all_to_all(
        jnp.broadcast_to(value[None], (count, *value.shape)), axis, 0, 0, tiled=True
    )


def gather_directly(value, axis, dim):
    return in_order(from_everyone(value, axis), dim)


def passed_along(block, axis, distance):
    devices = range(lax.axis_size(axis))
    route = [(i - distance, i) for i in devices if i - distance in devices]
    return lax.ppermute(block, axis, route)


def spread_panel(panel):
    return lax.all_gather(panel, "col", axis=0, tiled=True)


def row_partials(make_terms, keep_rows):
    return summed_on_arrival(
        make_terms(jnp.int32(0), keep_rows * lax.axis_size("row")).astype(jnp.bfloat16), "row", 0
    )


def layer_backward(x_local, dy_local, w_both, w_down):
    hidden_width = w_down.shape[0]
    x_whole = spread_panel(x_local)
    dy_whole = spread_panel(dy_local)
    keep_rows = x_whole.shape[0] // lax.axis_size("row")

    def forward_terms(first_row, row_count):
        return jnp.dot(x_whole, w_both, preferred_element_type=jnp.float32)

    def backward_terms(first_row, row_count):
        return lax.dot_general(dy_whole, w_down, CONTRACT_COLS, preferred_element_type=jnp.float32)

    both_sums = row_partials(forward_terms, keep_rows)
    hidden_grad = row_partials(backward_terms, keep_rows)
    gate_sum = both_sums[:, :hidden_width]
    up_sum = both_sums[:, hidden_width:]
    sigmoid_gate = jax.nn.sigmoid(gate_sum)
    activated = gate_sum * sigmoid_gate
    slope = sigmoid_gate * (1.0 + gate_sum * (1.0 - sigmoid_gate))
    hidden = (activated * up_sum).astype(jnp.bfloat16)
    gate_grad = (hidden_grad * up_sum * slope).astype(jnp.bfloat16)
    up_grad = (hidden_grad * activated).astype(jnp.bfloat16)
    packed = jnp.concatenate([hidden, gate_grad, up_grad], axis=1)
    gathered = gather_directly(packed, "row", 0)
    hidden_whole = gathered[:, :hidden_width]
    both_grads = gathered[:, hidden_width:]
    branch_sum = summed_on_arrival(
        lax.dot_general(
            both_grads, w_both, CONTRACT_COLS, preferred_element_type=jnp.float32
        ).astype(jnp.bfloat16),
        "col",
        0,
    )
    input_grad = (dy_local.astype(jnp.float32) + branch_sum).astype(jnp.bfloat16)
    down_update = lax.dot_general(
        hidden_whole, dy_whole, CONTRACT_ROWS, preferred_element_type=jnp.float32
    )
    both_update = lax.dot_general(
        x_whole, both_grads, CONTRACT_ROWS, preferred_element_type=jnp.float32
    )
    return (input_grad, both_update, down_update)


def shards(section_inputs, out_grad, gate_weight, up_weight, down_weight):
    section_id = lax.axis_index("section")
    last_section = lax.axis_size("section") - 1
    is_last = section_id == last_section
    panels = section_inputs[0]
    w_both = jnp.concatenate([gate_weight[0], up_weight[0]], axis=1)
    w_down = down_weight[0]
    hidden_width = w_down.shape[0]
    micro_count = panels.shape[0]
    both_total = jnp.zeros(w_both.shape, jnp.float32)
    down_total = jnp.zeros(w_down.shape, jnp.float32)
    merged_shape = (micro_count * panels.shape[1], panels.shape[2])
    x_local = panels.reshape(merged_shape)
    top_grads = out_grad.reshape(merged_shape)
    received = jnp.zeros(merged_shape, jnp.bfloat16)
    merged_results = received
    for step_index in range(last_section + 1):
        is_active = section_id == last_section - step_index
        dy_local = jnp.where(is_last, top_grads, received)
        input_grad, both_update, down_update = layer_backward(x_local, dy_local, w_both, w_down)
        merged_results = jnp.where(is_active, input_grad, merged_results)
        both_total = both_total + jnp.where(is_active, both_update, 0.0)
        down_total = down_total + jnp.where(is_active, down_update, 0.0)
        if step_index < last_section:
            received = passed_along(input_grad, "section", -1)
    results = merged_results.reshape(panels.shape)
    return (
        results[None],
        both_total[:, :hidden_width][None],
        both_total[:, hidden_width:][None],
        down_total[None],
    )


def solution(mesh):
    return jax.shard_map(
        shards,
        mesh=mesh,
        in_specs=(
            P("section", None, "col", "row"),
            P(None, "col", "row"),
            P("section", "row", "col"),
            P("section", "row", "col"),
            P("section", "col", "row"),
        ),
        out_specs=(
            P("section", None, "col", "row"),
            P("section", "row", "col"),
            P("section", "row", "col"),
            P("section", "col", "row"),
        ),
        check_vma=False,
    )
```

profile of v0, /device:TPU:32, one launch (start us, length us, event | category | flops | bytes accessed | tf_op | source)
XLA Modules:
  0.0 293.4 jit_solution(17711729461462888270)
XLA Ops:
  0.7 0.8 bitcast_select_fusion.1
  1.5 27.4 %all_gather.11 = bf16[384,256]{1,0:T(8,128)(2,1)S(1)} all-gather(bf16[48,256]{1,0:T(8,128)(2,1)S(1)} %bitcast_select_fusion.1), channel_id=1, replica_groups=mesh['section'=2,'row'=16,'col'=8] {'col'}, dimensions={0}, use_global_device_ids=true | all-gather | bytes 221184 | tf_op jit(solution)/shard_map/all_gather | solution.py:45
  28.9 0.7 copy-done.6
  29.6 1.6 convolution_convert_fusion.2
  31.2 7.0 %all-to-all-start.1 = ((bf16[16,24,1792]{2,1,0:T(8,128)(2,1)}), bf16[16,24,1792]{2,1,0:T(8,128)(2,1)S(1)}, u32[]{:S(2)}, u32[]{:S(2)}) async-start(bf16[16,24,1792]{2,1,0:T(8,128)(2,1)} %bitcast.42), calls=%async_computation.1 | async-start | bytes 2752512 | tf_op jit(solution)/shard_map/all_to_all | solution.py:17
  38.3 24.7 %all_gather.10 = bf16[384,256]{1,0:T(8,128)(2,1)S(1)} all-gather(bf16[48,256]{1,0:T(8,128)(2,1)S(1)} %bitcast.51), channel_id=1, replica_groups=mesh['section'=2,'row'=16,'col'=8] {'col'}, dimensions={0}, use_global_device_ids=true | all-gather | bytes 221184 | tf_op jit(solution)/shard_map/all_gather | solution.py:45
  62.9 3.7 %convolution_convert_fusion = bf16[3584,384]{0,1:T(8,128)(2,1)} fusion(bf16[384,256]{1,0:T(8,128)(2,1)S(1)} %all_gather.10, bf16[256,1792]{1,0:T(8,128)(2,1)S(1)} %bitcast.44, bf16[256,1792]{1,0:T(8,128)(2,1)} %bitcast.47), kind=kOutput, calls=%fused_computation | convolution fusion | flops 709689344 | bytes 4784128 | tf_op jit(solution)/shard_map/dot_general | solution.py:61
  66.6 7.3 %all-to-all-start = ((bf16[16,24,3584]{2,1,0:T(8,128)(2,1)}), bf16[16,24,3584]{2,1,0:T(8,128)(2,1)}, u32[]{:S(2)}, u32[]{:S(2)}) async-start(bf16[16,24,3584]{2,1,0:T(8,128)(2,1)} %bitcast.41), calls=%async_computation | async-start | bytes 5505024 | tf_op jit(solution)/shard_map/all_to_all | solution.py:17
  73.9 0.9 convert_reduce_fusion.2
  74.7 26.4 %all-to-all-done = bf16[16,24,3584]{2,1,0:T(8,128)(2,1)} async-done(((bf16[16,24,3584]{2,1,0:T(8,128)(2,1)}), bf16[16,24,3584]{2,1,0:T(8,128)(2,1)}, u32[]{:S(2)}, u32[]{:S(2)}) %all-to-all-start) | async-done | bytes 2752544 | tf_op jit(solution)/shard_map/all_to_all | solution.py:17
  101.2 2.2 convert_reduce_fusion
  103.8 44.6 %all_to_all.36 = bf16[16,24,5376]{2,1,0:T(8,128)(2,1)S(1)} all-to-all(bf16[16,24,5376]{2,1,0:T(8,128)(2,1)S(1)} %broadcast_in_dim.35), channel_id=1, replica_groups=mesh['section'=2,'row'=16,'col'=8] {'row'}, dimensions={0} | all-to-all | bytes 8257536 | tf_op jit(solution)/shard_map/all_to_all | solution.py:29
  148.4 0.9 fusion.12
  149.3 1.0 copy-done.1
  150.4 14.0 %all_to_all.37 = bf16[8,48,256]{2,1,0:T(8,128)(2,1)S(1)} all-to-all(bf16[8,48,256]{2,1,0:T(8,128)(2,1)S(1)} %bitcast.50), channel_id=1, replica_groups=mesh['section'=2,'row'=16,'col'=8] {'col'}, dimensions={0} | all-to-all | bytes 393216 | tf_op jit(solution)/shard_map/all_to_all | solution.py:17
  164.4 1.3 collective-permute-start
  165.7 1.8 collective-permute-done
  167.5 23.6 %all_gather.12 = bf16[384,256]{1,0:T(8,128)(2,1)S(1)} all-gather(bf16[48,256]{1,0:T(8,128)(2,1)S(1)} %bitcast_select_fusion), channel_id=1, replica_groups=mesh['section'=2,'row'=16,'col'=8] {'col'}, dimensions={0}, use_global_device_ids=true | all-gather | bytes 221184 | tf_op jit(solution)/shard_map/all_gather | solution.py:45
  191.6 17.9 %all_to_all.38 = bf16[16,24,1792]{2,1,0:T(8,128)(2,1)S(1)} all-to-all(bf16[16,24,1792]{2,1,0:T(8,128)(2,1)S(1)} %bitcast.43), channel_id=1, replica_groups=mesh['section'=2,'row'=16,'col'=8] {'row'}, dimensions={0} | all-to-all | bytes 2752512 | tf_op jit(solution)/shard_map/all_to_all | solution.py:17
  209.9 2.2 broadcast_in_dim.36
  212.1 4.7 %all-to-all-start.5 = ((bf16[16,24,5376]{2,1,0:T(8,128)(2,1)}), bf16[16,24,5376]{2,1,0:T(8,128)(2,1)}, u32[]{:S(2)}, u32[]{:S(2)}) async-start(bf16[16,24,5376]{2,1,0:T(8,128)(2,1)} %broadcast_in_dim.36), calls=%async_computation.5 | async-start | bytes 8257536 | tf_op jit(solution)/shard_map/all_to_all | solution.py:29
  216.8 3.4 %convolution_select_fusion.3 = f32[1792,256]{1,0:T(8,128)} fusion(bf16[384,256]{1,0:T(8,128)(2,1)S(1)} %copy-done.7, bf16[384,5376]{1,0:T(8,128)(2,1)} %bitcast.39, pred[]{:T(512)S(6)} %eq.8), kind=kOutput, calls=%fused_computation.9 | convolution fusion | flops 352780288 | bytes 3407873 | tf_op jit(solution)/shard_map/dot_general | solution.py:88
  220.1 45.0 %all-to-all-done.5 = bf16[16,24,5376]{2,1,0:T(8,128)(2,1)} async-done(((bf16[16,24,5376]{2,1,0:T(8,128)(2,1)}), bf16[16,24,5376]{2,1,0:T(8,128)(2,1)}, u32[]{:S(2)}, u32[]{:S(2)}) %all-to-all-start.5) | async-done | bytes 4128800 | tf_op jit(solution)/shard_map/all_to_all | solution.py:29
  265.1 3.6 %fusion.15 = bf16[384,256]{1,0:T(8,128)(2,1)} fusion(bf16[384,5376]{1,0:T(8,128)(2,1)} %bitcast.11, bf16[256,1792]{1,0:T(8,128)(2,1)S(1)} %bitcast.46, bf16[256,1792]{1,0:T(8,128)(2,1)} %bitcast.48), kind=kOutput, calls=%fused_computation.26 | convolution fusion | flops 708411392 | bytes 4784128 | tf_op jit(solution)/shard_map/dot_general | solution.py:81
  268.7 3.1 %convolution_select_fusion = f32[3584,256]{1,0:T(8,128)S(1)} fusion(bf16[384,256]{1,0:T(8,128)(2,1)S(1)} %all_gather.10, bf16[384,5376]{1,0:T(8,128)(2,1)} %bitcast.11, pred[]{:T(512)S(6)} %eq.7), kind=kOutput, calls=%fused_computation.1 | convolution fusion | flops 705560576 | bytes 6619137 | tf_op jit(solution)/shard_map/dot_general | solution.py:91
  271.8 3.0 %fusion.1 = f32[256,3584]{0,1:T(8,128)} fusion(f32[3584,256]{1,0:T(8,128)S(1)} %convolution_select_fusion, bf16[384,256]{1,0:T(8,128)(2,1)S(1)} %all_gather.10, bf16[384,5376]{1,0:T(8,128)(2,1)S(1)} %bitcast.40, pred[]{:T(512)S(6)} %eq.8), kind=kOutput, calls=%fused_computation.5 | convolution fusion | flops 706478080 | bytes 10289153 | tf_op jit(solution)/shard_map/dot_general | solution.py:91
  274.8 6.2 %all-to-all-start.6 = ((bf16[8,48,256]{2,1,0:T(8,128)(2,1)}), bf16[8,48,256]{2,1,0:T(8,128)(2,1)S(1)}, u32[]{:S(2)}, u32[]{:S(2)}) async-start(bf16[8,48,256]{2,1,0:T(8,128)(2,1)} %bitcast.12), calls=%async_computation.6 | async-start | bytes 393216 | tf_op jit(solution)/shard_map/all_to_all | solution.py:17
  281.0 3.5 %slice_bitcast_fusion = (f32[1,256,1792]{1,2,0:T(8,128)}, f32[1,256,1792]{1,2,0:T(8,128)S(1)}) fusion(f32[256,3584]{0,1:T(8,128)} %fusion.1), kind=kLoop, calls=%fused_computation.20 | loop fusion | bytes 7340032 | tf_op jit(solution)/shard_map/broadcast_in_dim | solution.py:126
  284.5 2.7 copy.10
  287.2 1.7 copy.9
  288.9 3.8 %fusion.3 = f32[1,1792,256]{2,1,0:T(8,128)} fusion(f32[1792,256]{1,0:T(8,128)} %convolution_select_fusion.3, bf16[384,256]{1,0:T(8,128)(2,1)S(1)} %all_gather.12, bf16[384,5376]{1,0:T(8,128)(2,1)} %bitcast.11, pred[]{:T(512)S(6)} %eq.7), kind=kOutput, calls=%fused_computation.13 | convolution fusion | flops 353239040 | bytes 5242881 | tf_op jit(solution)/shard_map/dot_general | solution.py:88
  292.8 0.6 fusion.23
  (33 shorter events, 1.4 us)
Async XLA Ops:
  0.6 28.9 %copy-start = (bf16[1,1792,256]{2,1,0:T(8,128)(2,1)S(1)}, bf16[1,1792,256]{2,1,0:T(8,128)(2,1)}, u32[]{:S(2)}) copy-start(bf16[1,1792,256]{2,1,0:T(8,128)(2,1)} %param.9) | copy-start | bytes 2752516
  0.7 37.6 %copy-start.10 = (bf16[1,2,24,256]{3,2,1,0:T(8,128)(2,1)S(1)}, bf16[1,2,24,256]{3,2,1,0:T(8,128)(2,1)}, u32[]{:S(2)}) copy-start(bf16[1,2,24,256]{3,2,1,0:T(8,128)(2,1)} %param.5) | copy-start | bytes 73732
  28.9 0.7 copy-start.6
  29.6 33.4 %copy-start.3 = (bf16[1,256,1792]{2,1,0:T(8,128)(2,1)S(1)}, bf16[1,256,1792]{2,1,0:T(8,128)(2,1)}, u32[]{:S(2)}) copy-start(bf16[1,256,1792]{2,1,0:T(8,128)(2,1)} %param.8) | copy-start | bytes 2752516
  31.2 35.4 %all-to-all-start.1 = ((bf16[16,24,1792]{2,1,0:T(8,128)(2,1)}), bf16[16,24,1792]{2,1,0:T(8,128)(2,1)S(1)}, u32[]{:S(2)}, u32[]{:S(2)}) async-start(bf16[16,24,1792]{2,1,0:T(8,128)(2,1)} %bitcast.42), calls=%async_computation.1 | async-start | bytes 2752512 | tf_op jit(solution)/shard_map/all_to_all | solution.py:17
  66.6 34.5 %all-to-all-start = ((bf16[16,24,3584]{2,1,0:T(8,128)(2,1)}), bf16[16,24,3584]{2,1,0:T(8,128)(2,1)}, u32[]{:S(2)}, u32[]{:S(2)}) async-start(bf16[16,24,3584]{2,1,0:T(8,128)(2,1)} %bitcast.41), calls=%async_computation | async-start | bytes 5505024 | tf_op jit(solution)/shard_map/all_to_all | solution.py:17
  74.7 28.6 %copy-start.8 = (f32[24,1792]{1,0:T(8,128)S(1)}, f32[24,1792]{1,0:T(8,128)}, u32[]{:S(2)}) copy-start(f32[24,1792]{1,0:T(8,128)} %convert_reduce_fusion.2) | copy-start | bytes 516100
  103.8 44.6 %copy-start.5 = (bf16[1,256,1792]{2,1,0:T(8,128)(2,1)S(1)}, bf16[1,256,1792]{2,1,0:T(8,128)(2,1)}, u32[]{:S(2)}) copy-start(bf16[1,256,1792]{2,1,0:T(8,128)(2,1)} %param.7) | copy-start | bytes 2752516
  148.4 1.9 copy-start.1
  148.4 15.9 %copy-start.9 = (bf16[2,24,256]{2,1,0:T(8,128)(2,1)S(1)}, bf16[2,24,256]{2,1,0:T(8,128)(2,1)}, u32[]{:S(2)}) copy-start(bf16[2,24,256]{2,1,0:T(8,128)(2,1)} %param.6) | copy-start | bytes 73732
  164.4 3.1 %collective-permute-start = (bf16[48,256]{1,0:T(8,128)(2,1)S(1)}, bf16[48,256]{1,0:T(8,128)(2,1)S(1)}, u32[]{:S(2)}, u32[]{:S(2)}) collective-permute-start(bf16[48,256]{1,0:T(8,128)(2,1)S(1)} %add_convert_fusion.1), channel_id=1, source_target_pairs={{128,0},{129,1},{130,2},{131,3},{132,4},{133,5},{134,6},{135,7},{1... | collective-permute-start | bytes 73736 | tf_op jit(solution)/shard_map/ppermute | solution.py:41
  212.1 4.7 %copy-start.7 = (bf16[384,256]{1,0:T(8,128)(2,1)S(1)}, bf16[384,256]{1,0:T(8,128)(2,1)}, u32[]{:S(2)}) copy-start(bf16[384,256]{1,0:T(8,128)(2,1)} %copy-done.6) | copy-start | bytes 589828
  212.1 53.0 %all-to-all-start.5 = ((bf16[16,24,5376]{2,1,0:T(8,128)(2,1)}), bf16[16,24,5376]{2,1,0:T(8,128)(2,1)}, u32[]{:S(2)}, u32[]{:S(2)}) async-start(bf16[16,24,5376]{2,1,0:T(8,128)(2,1)} %broadcast_in_dim.36), calls=%async_computation.5 | async-start | bytes 8257536 | tf_op jit(solution)/shard_map/all_to_all | solution.py:29
  216.7 48.4 %copy-start.4 = (bf16[1,256,1792]{2,1,0:T(8,128)(2,1)S(1)}, bf16[1,256,1792]{2,1,0:T(8,128)(2,1)}, u32[]{:S(2)}) copy-start(bf16[1,256,1792]{2,1,0:T(8,128)(2,1)} %param.8) | copy-start | bytes 2752516
  268.7 3.1 %copy-start.2 = (bf16[16,24,5376]{2,1,0:T(8,128)(2,1)S(1)}, bf16[16,24,5376]{2,1,0:T(8,128)(2,1)}, u32[]{:S(2)}) copy-start(bf16[16,24,5376]{2,1,0:T(8,128)(2,1)} %copy-done.1) | copy-start | bytes 12386308
  274.8 17.9 %all-to-all-start.6 = ((bf16[8,48,256]{2,1,0:T(8,128)(2,1)}), bf16[8,48,256]{2,1,0:T(8,128)(2,1)S(1)}, u32[]{:S(2)}, u32[]{:S(2)}) async-start(bf16[8,48,256]{2,1,0:T(8,128)(2,1)} %bitcast.12), calls=%async_computation.6 | async-start | bytes 393216 | tf_op jit(solution)/shard_map/all_to_all | solution.py:17
where the time goes:
time: 294 us; the launch traced here: 293 us
  blocking collectives  152 us (52%)
  waiting for transfers between devices  73.2 us (25%)
  starting transfers between devices  26.4 us (9%)
  matrix products  23.6 us (8%)
  local copies, waits for them, and re-layouts  12.1 us (4%)
  other arithmetic  5.01 us (2%)
    all_gather x3, blocking collectives, spread_panel(): return lax.all_gather(panel, 'col', axis=0, tiled=True)  75.6 us
    all_to_all x1, waiting for transfers between devices, from_everyone(): lax.all_to_all(jnp.broadcast_to(value[None], (count, *value.shape)), axis...  45 us
    all_to_all x1, blocking collectives, from_everyone(): lax.all_to_all(jnp.broadcast_to(value[None], (count, *value.shape)), axis...  44.6 us
    all_to_all x2, blocking collectives, summed_on_arrival(): lax.all_to_all(cut_along(value, dim, count), axis, 0, 0, tiled=True)  31.9 us
    all_to_all x3, waiting for transfers between devices, summed_on_arrival(): lax.all_to_all(cut_along(value, dim, count), axis, 0, 0, tiled=True)  26.4 us
    all_to_all x3, starting transfers between devices, summed_on_arrival(): lax.all_to_all(cut_along(value, dim, count), axis, 0, 0, tiled=True)  20.5 us
    dot_general x2, matrix products, layer_backward(): lax.dot_general(hidden_whole, dy_whole, CONTRACT_ROWS, preferred_element_...  7.2 us
    unnamed x24, local copies, waits for them, and re-layouts  6.14 us
  transfers between devices with their start and end apart: 5, of which 3 were waited for; matrix products, arithmetic and copies ran while one was open for 7% of the time, Pallas kernels for 0%

commit v1 on v0

v1 whole, which is shorter than its diff:
```python
import functools

import jax
import jax.numpy as jnp
from jax import lax
from jax.experimental import pallas as pl
from jax.experimental.pallas import tpu as pltpu
from jax.sharding import PartitionSpec as P

MESH = pl.DeviceIdType.MESH
BF16 = jnp.bfloat16
F32 = jnp.float32
RING = 4
GATE, UP, DHID = 0, 1, 2
HIDDEN, DGATE, DUP = 0, 1, 2
NT_DIMS = (((1,), (1,)), ((), ()))
TN_DIMS = (((0,), (0,)), ((), ()))


def relay_kernel(
    n_col,
    x_ref, dy_ref, wg_hbm, wu_hbm, wd_hbm,
    out_ref, h_hbm, xall_hbm, dyall_hbm,
    wg, wu, wd, xall, dyall, part, ra, rb, ra2, rb2, final, gath, factors, acc, dxp, rz, blk_out,
    load_sem, store_sem,
    rs_send, rs_recv, ag_send, ag_recv, zx_send, zx_recv, zy_send, zy_recv, zr_send, zr_recv, zo_send, zo_recv,
):
    sec = lax.axis_index("section")
    row = lax.axis_index("row")
    col = lax.axis_index("col")
    gx = lax.rem(row, RING)
    gy = lax.div(row, RING)
    tok_loc = x_ref.shape[0]
    tok = xall.shape[0]
    tiles = wg.shape[1] // 256
    blk = tok // RING
    sub = blk // RING
    half = blk // 2
    ta = (tiles + 1) // 2

    def step(pos, d):
        return lax.rem(pos + (d + RING), RING)

    def along_x(d):
        return (sec, gy * RING + step(gx, d), col)

    def along_y(d):
        return (sec, step(gy, d) * RING + gx, col)

    def z_peer(d):
        return lax.rem(col + d, n_col)

    pos1 = (gx, gy)
    pos2 = (gy, gx)
    ring1 = (along_x, along_y)
    ring2 = (along_y, along_x)

    weights = ((wg_hbm, wg), (wu_hbm, wu), (wd_hbm, wd))
    loads = [pltpu.make_async_copy(s, d, load_sem.at[i]) for i, (s, d) in enumerate(weights)]
    for c in loads:
        c.start()

    barrier = pltpu.get_barrier_semaphore()
    greeted = [along_x(1), along_x(-1), along_y(1), along_y(-1)]
    greeted += [(sec, row, z_peer(d)) for d in range(1, n_col)]
    greeted += [(1 - sec, row, z_peer(d)) for d in range(n_col)]
    for dev in greeted:
        pl.semaphore_signal(barrier, inc=1, device_id=dev, device_id_type=MESH)
    pl.semaphore_wait(barrier, len(greeted))

    def rcopy(src, dst, ssem, rsem, dev):
        return pltpu.make_async_remote_copy(
            src_ref=src, dst_ref=dst, send_sem=ssem, recv_sem=rsem, device_id=dev, device_id_type=MESH
        )

    def aligned(v, m=8):
        return pl.multiple_of(v, m)

    my_rows = pl.ds(aligned(col * tok_loc), tok_loc)

    def spread(src, dst, ssem, rsem):
        sent = []
        for d in range(1, n_col):
            c = rcopy(src, dst.at[my_rows, :], ssem.at[d], rsem.at[d], (sec, row, z_peer(d)))
            c.start()
            sent.append(c)
        return sent

    def region1(ref, k, h, q, part_ab):
        return ref.at[k, h, :, pl.ds(aligned(q * blk + part_ab * half), half), :]

    def region2(ref, k, h, q, part_ab):
        t = pl.ds(0, ta) if part_ab == 0 else pl.ds(ta, tiles - ta)
        return ref.at[k, h, t, pl.ds(aligned(pos1[h] * blk + q * sub), sub), :]

    def recv1(k, h, way, part_ab):
        return rb.at[k, h, way, :, pl.ds(part_ab * half, half), :]

    def recv2(k, h, way, part_ab):
        t = pl.ds(0, ta) if part_ab == 0 else pl.ds(ta, tiles - ta)
        return rb2.at[k, h, way, t, :, :]

    def early1(k, h, way):
        return ra.at[k, h, way]

    def early2(k, h, way):
        t = pl.ds(0, ta) if way == 0 else pl.ds(ta, tiles - ta)
        return ra2.at[k, h, t, :, :]

    stages = (
        (pos1, ring1, region1, recv1, early1),
        (pos2, ring2, region2, recv2, early2),
    )

    def rs_copy(k, h, st, way, kind):
        pos, ring, region, recv, early = stages[st]
        d = 1 if way == 0 else -1
        ssem, rsem = rs_send.at[k, h, st, way, kind], rs_recv.at[k, h, st, way, kind]
        if kind == 0:
            src, dst = region(part, k, h, step(pos[h], 2), way), early(k, h, way)
        else:
            ab = way if kind == 2 else 1 - way
            src, dst = region(part, k, h, step(pos[h], d), ab), recv(k, h, way, ab)
        return rcopy(src, dst, ssem, rsem, ring[h](d))

    def rs_start(k, st):
        for kind in (0, 1):
            for h in range(2):
                for way in range(2):
                    rs_copy(k, h, st, way, kind).start()

    def add_into(dst, src):
        def body(t, _):
            dst[t] = (dst[t].astype(F32) + src[t].astype(F32)).astype(BF16)
            return 0

        lax.fori_loop(0, dst.shape[0], body, 0)

    def rs_mid(k, st):
        pos, ring, region, recv, early = stages[st]
        for h in range(2):
            for way in range(2):
                d = 1 if way == 0 else -1
                rs_copy(k, h, st, way, 0).wait_recv()
                add_into(region(part, k, h, step(pos[h], d), way), early(k, h, way))
                rs_copy(k, h, st, way, 2).start()

    def rs_wait(k, st):
        for h in range(2):
            for kind in (1, 2):
                for way in range(2):
                    rs_copy(k, h, st, way, kind).wait_recv()

    def rs_end1(k):
        rs_wait(k, 0)
        for h in range(2):
            own = part.at[k, h, :, pl.ds(aligned(pos1[h] * blk), blk), :]
            a, b = rb.at[k, h, 0], rb.at[k, h, 1]

            def body(t, _):
                own[t] = (own[t].astype(F32) + (a[t].astype(F32) + b[t].astype(F32))).astype(BF16)
                return 0

            lax.fori_loop(0, tiles, body, 0)

    def piece(ref, k, h):
        return ref.at[k, h, :, pl.ds(aligned(pos1[h] * blk + pos2[h] * sub), sub), :]

    def rs_end2(k):
        rs_wait(k, 1)
        for h in range(2):
            own, a, b, f = piece(part, k, h), rb2.at[k, h, 0], rb2.at[k, h, 1], final.at[k, h]

            def body(t, _):
                f[t] = own[t].astype(F32) + (a[t].astype(F32) + b[t].astype(F32))
                return 0

            lax.fori_loop(0, tiles, body, 0)

    def rs_drain(k):
        for st in range(2):
            for h in range(2):
                for way in range(2):
                    for kind in range(3):
                        rs_copy(k, h, st, way, kind).wait_send()

    def reduce_rows(ks):
        for k in ks:
            rs_mid(k, 0)
        for k in ks:
            rs_end1(k)
            rs_start(k, 1)
        for k in ks:
            rs_mid(k, 1)
        for k in ks:
            rs_end2(k)

    def ag_copy(k, h, st, way, kind):
        pos, ring, region, _, _ = stages[st]
        d = 1 if way == 0 else -1
        ssem, rsem = ag_send.at[k, h, st, way, kind], ag_recv.at[k, h, st, way, kind]
        ab = 1 - way if kind == 1 else way
        q = pos[h] if kind < 2 else step(pos[h], -d)
        ref = region(gath, k, h, q, ab)
        return rcopy(ref, ref, ssem, rsem, ring[h](d))

    def ag_start(k, st):
        for kind in (0, 1):
            for h in range(2):
                for way in range(2):
                    ag_copy(k, h, st, way, kind).start()

    def ag_mid(k, st):
        for h in range(2):
            for way in range(2):
                ag_copy(k, h, st, way, 0).wait_recv()
                ag_copy(k, h, st, way, 2).start()

    def ag_end(k, st):
        for h in range(2):
            for kind in (1, 2):
                for way in range(2):
                    ag_copy(k, h, st, way, kind).wait_recv()

    def ag_drain(k):
        for st in range(2):
            for h in range(2):
                for way in range(2):
                    for kind in range(3):
                        ag_copy(k, h, st, way, kind).wait_send()

    def gather_rows(ks):
        for k in ks:
            ag_start(k, 1)
        for k in ks:
            ag_mid(k, 1)
        for k in ks:
            ag_end(k, 1)
            ag_start(k, 0)
        for k in ks:
            ag_mid(k, 0)
        for k in ks:
            ag_end(k, 0)

    def partials(k):
        def body(t, _):
            cols = pl.ds(pl.multiple_of(t * 256, 256), 256)
            if k == DHID:
                o = lax.dot_general(dyall[...], wd[cols, :], NT_DIMS, preferred_element_type=F32)
            else:
                w = wg if k == GATE else wu
                o = jnp.dot(xall[...], w[:, cols], preferred_element_type=F32)
            part[k, 0, t] = o[:, :128].astype(BF16)
            part[k, 1, t] = o[:, 128:].astype(BF16)
            return 0

        lax.fori_loop(0, tiles, body, 0)

    def swiglu(gate, up):
        sig = 1.0 / (1.0 + jnp.exp(-gate))
        act = gate * sig
        return act, up * (sig * (1.0 + gate * (1.0 - sig)))

    def exchange_cols():
        sent = []
        for d in range(1, n_col):
            peer = z_peer(d)
            c = rcopy(
                dxp.at[pl.ds(aligned(peer * tok_loc), tok_loc), :], rz.at[d], zr_send.at[d], zr_recv.at[d], (sec, row, peer)
            )
            c.start()
            sent.append(c)
        total = acc[my_rows, :]
        for c in sent:
            c.wait_recv()
        for d in range(1, n_col):
            total = total + rz[d].astype(F32)
        return total, sent

    def copies_out(src):
        out = [
            pltpu.make_async_copy(src, h_hbm, store_sem.at[0]),
            pltpu.make_async_copy(xall, xall_hbm, store_sem.at[1]),
            pltpu.make_async_copy(dyall, dyall_hbm, store_sem.at[2]),
        ]
        for c in out:
            c.start()
        return out

    xall[my_rows, :] = x_ref[...]

    @pl.when(sec == 1)
    def _():
        dyall[my_rows, :] = dy_ref[...]
        sent = spread(dy_ref, dyall, zy_send, zy_recv)
        sent_x = spread(x_ref, xall, zx_send, zx_recv)
        for c in loads:
            c.wait()
        for c in sent:
            c.wait_recv()
        partials(DHID)
        rs_start(DHID, 0)
        for c in sent_x:
            c.wait_recv()
        for k in (GATE, UP):
            partials(k)
            rs_start(k, 0)
        reduce_rows((DHID, GATE, UP))
        for h in range(2):
            outs = [piece(gath, k, h) for k in range(3)]

            def body(t, _):
                gate, up, dhid = final[GATE, h, t], final[UP, h, t], final[DHID, h, t]
                act, slope = swiglu(gate, up)
                outs[HIDDEN][t] = (act * up).astype(BF16)
                outs[DGATE][t] = (dhid * slope).astype(BF16)
                outs[DUP][t] = (dhid * act).astype(BF16)
                return 0

            lax.fori_loop(0, tiles, body, 0)
        gather_rows((DGATE, DUP, HIDDEN))
        stored = copies_out(gath)
        acc[...] = jnp.zeros_like(acc)

        def body(t, _):
            cols = pl.ds(pl.multiple_of(t * 256, 256), 256)
            g = jnp.concatenate([gath[DGATE, 0, t], gath[DGATE, 1, t]], axis=1)
            u = jnp.concatenate([gath[DUP, 0, t], gath[DUP, 1, t]], axis=1)
            acc[...] += lax.dot_general(g, wg[:, cols], NT_DIMS, preferred_element_type=F32) + lax.dot_general(
                u, wu[:, cols], NT_DIMS, preferred_element_type=F32
            )
            return 0

        lax.fori_loop(0, tiles, body, 0)
        dxp[...] = acc[...].astype(BF16)
        total, sent_z = exchange_cols()
        result = (dy_ref[...].astype(F32) + total).astype(BF16)
        out_ref[...] = result
        blk_out[...] = result
        given = []
        for d in range(n_col):
            c = rcopy(blk_out, dyall.at[my_rows, :], zo_send.at[d], zo_recv.at[d], (0, row, z_peer(d)))
            c.start()
            given.append(c)
        for c in sent + sent_x + sent_z + given:
            c.wait_send()
        for k in range(3):
            rs_drain(k)
            ag_drain(k)
        for c in stored:
            c.wait()

    @pl.when(sec == 0)
    def _():
        sent_x = spread(x_ref, xall, zx_send, zx_recv)
        for c in loads:
            c.wait()
        for c in sent_x:
            c.wait_recv()
        for k in (GATE, UP):
            partials(k)
            rs_start(k, 0)
        reduce_rows((GATE, UP))
        for k in (GATE, UP):
            for h in range(2):
                own = piece(gath, k, h)

                def body(t, _):
                    own[t] = final[k, h, t].astype(BF16)
                    return 0

                lax.fori_loop(0, tiles, body, 0)
        gather_rows((GATE, UP))
        for k in (GATE, UP):
            rs_drain(k)

        for h in range(2):

            def body(t, _):
                gate, up = gath[GATE, h, t].astype(F32), gath[UP, h, t].astype(F32)
                act, slope = swiglu(gate, up)
                part[HIDDEN, h, t] = (act * up).astype(BF16)
                factors[0, h, t] = slope
                factors[1, h, t] = act
                return 0

            lax.fori_loop(0, tiles, body, 0)

        for d in range(n_col):
            rcopy(blk_out, dyall.at[my_rows, :], zo_send.at[d], zo_recv.at[d], (0, row, z_peer(1))).wait_recv()
        partials(DHID)
        rs_start(DHID, 0)
        reduce_rows((DHID,))
        for h in range(2):
            own = piece(gath, DHID, h)

            def body(t, _):
                own[t] = final[DHID, h, t].astype(BF16)
                return 0

            lax.fori_loop(0, tiles, body, 0)
        gather_rows((DHID,))
        rs_drain(DHID)
        acc[...] = jnp.zeros_like(acc)

        def body(t, _):
            cols = pl.ds(pl.multiple_of(t * 256, 256), 256)
            gs, us = [], []
            for h in range(2):
                dh = gath[DHID, h, t].astype(F32)
                gs.append((dh * factors[0, h, t]).astype(BF16))
                us.append((dh * factors[1, h, t]).astype(BF16))
                part[DGATE, h, t] = gs[h]
                part[DUP, h, t] = us[h]
            g = jnp.concatenate(gs, axis=1)
            u = jnp.concatenate(us, axis=1)
            acc[...] += lax.dot_general(g, wg[:, cols], NT_DIMS, preferred_element_type=F32) + lax.dot_general(
                u, wu[:, cols], NT_DIMS, preferred_element_type=F32
            )
            return 0

        lax.fori_loop(0, tiles, body, 0)
        dxp[...] = acc[...].astype(BF16)
        stored = copies_out(part)
        total, sent_z = exchange_cols()
        out_ref[...] = (dyall[my_rows, :].astype(F32) + total).astype(BF16)
        for c in sent_x + sent_z:
            c.wait_send()
        for k in range(3):
            ag_drain(k)
        for c in stored:
            c.wait()


def relay(n_col, x, dy, wg, wu, wd):
    tok_loc, d_loc = x.shape
    f_loc = wg.shape[1]
    tok = tok_loc * n_col
    tiles = f_loc // 256
    blk = tok // RING
    sub = blk // RING
    sem = pltpu.SemaphoreType.DMA
    any_spec = pl.BlockSpec(memory_space=pltpu.HBM)
    vmem_spec = pl.BlockSpec(memory_space=pltpu.VMEM)
    return pl.pallas_call(
        functools.partial(relay_kernel, n_col),
        out_shape=(
            jax.ShapeDtypeStruct((tok_loc, d_loc), BF16),
            jax.ShapeDtypeStruct((3, 2, tiles, tok, 128), BF16),
            jax.ShapeDtypeStruct((tok, d_loc), BF16),
            jax.ShapeDtypeStruct((tok, d_loc), BF16),
        ),
        in_specs=[vmem_spec, vmem_spec, any_spec, any_spec, any_spec],
        out_specs=(vmem_spec, any_spec, any_spec, any_spec),
        scratch_shapes=[
            pltpu.VMEM((d_loc, f_loc), BF16),
            pltpu.VMEM((d_loc, f_loc), BF16),
            pltpu.VMEM((f_loc, d_loc), BF16),
            pltpu.VMEM((tok, d_loc), BF16),
            pltpu.VMEM((tok, d_loc), BF16),
            pltpu.VMEM((3, 2, tiles, tok, 128), BF16),
            pltpu.VMEM((3, 2, 2, tiles, blk // 2, 128), BF16),
            pltpu.VMEM((3, 2, 2, tiles, blk, 128), BF16),
            pltpu.VMEM((3, 2, tiles, sub, 128), BF16),
            pltpu.VMEM((3, 2, 2, tiles, sub, 128), BF16),
            pltpu.VMEM((3, 2, tiles, sub, 128), F32),
            pltpu.VMEM((3, 2, tiles, tok, 128), BF16),
            pltpu.VMEM((2, 2, tiles, tok, 128), F32),
            pltpu.VMEM((tok, d_loc), F32),
            pltpu.VMEM((tok, d_loc), BF16),
            pltpu.VMEM((n_col, tok_loc, d_loc), BF16),
            pltpu.VMEM((tok_loc, d_loc), BF16),
            sem((3,)),
            sem((3,)),
            sem((3, 2, 2, 2, 3)),
            sem((3, 2, 2, 2, 3)),
            sem((3, 2, 2, 2, 3)),
            sem((3, 2, 2, 2, 3)),
            sem((n_col,)),
            sem((n_col,)),
            sem((n_col,)),
            sem((n_col,)),
            sem((n_col,)),
            sem((n_col,)),
            sem((n_col,)),
            sem((n_col,)),
        ],
        compiler_params=pltpu.CompilerParams(
            collective_id=0, has_side_effects=True, vmem_limit_bytes=48 * 1024 * 1024
        ),
        name="relay",
    )(x, dy, wg, wu, wd)


def weight_kernel(h_ref, x_ref, dy_ref, gate_ref, up_ref, down_ref):
    hid = jnp.concatenate([h_ref[HIDDEN, 0, 0], h_ref[HIDDEN, 1, 0]], axis=1)
    g = jnp.concatenate([h_ref[DGATE, 0, 0], h_ref[DGATE, 1, 0]], axis=1)
    u = jnp.concatenate([h_ref[DUP, 0, 0], h_ref[DUP, 1, 0]], axis=1)
    gate_ref[...] = lax.dot_general(x_ref[...], g, TN_DIMS, preferred_element_type=F32)
    up_ref[...] = lax.dot_general(x_ref[...], u, TN_DIMS, preferred_element_type=F32)
    down_ref[...] = lax.dot_general(hid, dy_ref[...], TN_DIMS, preferred_element_type=F32)


def weight_grads(h, x, dy):
    tiles, tok = h.shape[2:4]
    d_loc = x.shape[1]
    whole = pl.BlockSpec((tok, d_loc), lambda t: (0, 0))
    wide = pl.BlockSpec((d_loc, 256), lambda t: (0, t))
    return pl.pallas_call(
        weight_kernel,
        grid=(tiles,),
        out_shape=(
            jax.ShapeDtypeStruct((d_loc, tiles * 256), F32),
            jax.ShapeDtypeStruct((d_loc, tiles * 256), F32),
            jax.ShapeDtypeStruct((tiles * 256, d_loc), F32),
        ),
        in_specs=[pl.BlockSpec((3, 2, 1, tok, 128), lambda t: (0, 0, t, 0, 0)), whole, whole],
        out_specs=(wide, wide, pl.BlockSpec((256, d_loc), lambda t: (t, 0))),
        name="weight_grads",
    )(h, x, dy)


def shards(section_inputs, out_grad, gate_weight, up_weight, down_weight):
    n_col = lax.axis_size("col")
    panels = section_inputs[0]
    merged = (panels.shape[0] * panels.shape[1], panels.shape[2])
    x = panels.reshape(merged)
    dy = out_grad.reshape(merged)
    out, h, x_all, dy_all = relay(n_col, x, dy, gate_weight[0], up_weight[0], down_weight[0])
    gate, up, down = weight_grads(h, x_all, dy_all)
    return out.reshape(panels.shape)[None], gate[None], up[None], down[None]


def solution(mesh):
    return jax.shard_map(
        shards,
        mesh=mesh,
        in_specs=(
            P("section", None, "col", "row"),
            P(None, "col", "row"),
            P("section", "row", "col"),
            P("section", "row", "col"),
            P("section", "col", "row"),
        ),
        out_specs=(
            P("section", None, "col", "row"),
            P("section", "row", "col"),
            P("section", "row", "col"),
            P("section", "col", "row"),
        ),
        check_vma=False,
    )
```

time: 294 us -> 137 us (0.47)
  blocking collectives: 152 us -> 0 us
  Pallas kernels: 0 us -> 127 us
  waiting for transfers between devices: 73.2 us -> 0 us
  starting transfers between devices: 26.4 us -> 0 us
  matrix products: 23.6 us -> 0 us
  local copies, waits for them, and re-layouts: 12.1 us -> 6.95 us
  other arithmetic: 5.01 us -> 0 us
    pallas_call x0 -> x2, Pallas kernels: none -> 127 us  [the longest x1 120 us: relay(): pl.pallas_call(functools.partial(relay_kernel, n_col), out_shape=(jax.Sha...]
    all_to_all x3 -> x0, blocking collectives: 76.5 us -> none  [the longest x1 44.6 us: from_everyone(): lax.all_to_all(jnp.broadcast_to(value[None], (count, *value.shape)), axis...]
    all_gather x3 -> x0, blocking collectives: 75.6 us -> none  [spread_panel(): return lax.all_gather(panel, 'col', axis=0, tiled=True)]
    all_to_all x4 -> x0, waiting for transfers between devices: 71.4 us -> none  [the longest x1 45 us: from_everyone(): lax.all_to_all(jnp.broadcast_to(value[None], (count, *value.shape)), axis...]
    all_to_all x4 -> x0, starting transfers between devices: 25.2 us -> none  [the longest x3 20.5 us: summed_on_arrival(): lax.all_to_all(cut_along(value, dim, count), axis, 0, 0, tiled=True)]
    dot_general x9 -> x0, matrix products: 23.6 us -> none  [the longest x2 7.2 us: layer_backward(): lax.dot_general(hidden_whole, dy_whole, CONTRACT_ROWS, preferred_element_...]
    broadcast_in_dim x3 -> x0, local copies, waits for them, and re-layouts: 6 us -> none  [the longest x1 3.52 us: shards(): both_total[:, hidden_width:][None]]
    reduce_sum x5 -> x0, other arithmetic: 3.28 us -> none  [summed_on_arrival(): return jnp.sum(pieces.astype(jnp.float32), axis=0)]
  transfers between devices with their start and end apart: 5 -> 0, of which waited for: 3 -> 0; matrix products, arithmetic and copies ran while one was open for 7% -> 0% of each run, Pallas kernels for 0% -> 0%
where the time goes in v1:
time: 137 us; the launch traced here: 135 us
  Pallas kernels  127 us (93%)
  local copies, waits for them, and re-layouts  6.95 us (5%)
    pallas_call x1, Pallas kernels, relay(): pl.pallas_call(functools.partial(relay_kernel, n_col), out_shape=(jax.Sha...  120 us
    pallas_call x1, Pallas kernels, weight_grads(): pl.pallas_call(weight_kernel, grid=(tiles,), out_shape=(jax.ShapeDtypeStr...  7.55 us
    unnamed x15, local copies, waits for them, and re-layouts  6.95 us

profile of v1, /device:TPU:32, one launch (start us, length us, event | category | flops | bytes accessed | tf_op | source)
XLA Modules:
  0.0 135.1 jit_solution(3303712576085786369)
XLA Ops:
  0.6 0.0 copy-start
  0.6 1.2 copy-done
  1.8 0.0 copy-start.1
  1.8 1.2 copy-done.1
  3.0 0.0 copy-start.2
  3.0 1.2 copy-done.2
  4.2 0.0 copy-start.5
  4.2 0.7 copy-done.5
  4.9 0.0 copy-start.6
  4.9 0.7 copy-done.6
  5.6 119.9 %relay.1 = (bf16[48,256]{1,0:T(8,128)(2,1)S(1)}, bf16[3,2,7,384,128]{4,3,2,1,0:T(8,128)(2,1)}, bf16[384,256]{1,0:T(8,128)(2,1)S(1)}, bf16[384,256]{1,0:T(8,128)(2,1)S(1)}) custom-call(bf16[48,256]{1,0:T(8,128)(2,1)S(1)} %bitcast.12, bf16[48,256]{1,0:T(8,128)(2,1)S(1)} %bitcast.13, bf16[256,1792]{1,0:T(8,128)(2,1)S(1)} %bitcast.9, ...), custom_call_target="tpu_custom_call" | custom-call | tf_op jit(solution)/shard_map/relay/pallas_call | solution.py:445
  125.6 0.0 copy-start.3
  125.6 0.7 copy-done.3
  126.2 0.0 copy-start.4
  126.2 0.7 copy-done.4
  126.9 7.6 %weight_grads.1 = (f32[256,1792]{1,0:T(8,128)}, f32[256,1792]{1,0:T(8,128)}, f32[1792,256]{1,0:T(8,128)}) custom-call(bf16[3,2,7,384,128]{4,3,2,1,0:T(8,128)(2,1)} %get-tuple-element.12.h_ref, bf16[384,256]{1,0:T(8,128)(2,1)} %copy-done.3, bf16[384,256]{1,0:T(8,128)(2,1)} %copy-done.4), custom_call_target="tpu_custom_call" | custom-call | tf_op jit(solution)/shard_map/weight_grads/pallas_call | solution.py:509
  134.5 0.6 copy.10
Async XLA Ops:
  0.6 1.2 copy-start
  1.8 1.2 copy-start.1
  3.0 1.2 copy-start.2
  4.2 0.7 copy-start.5
  4.9 0.7 copy-start.6
  125.6 0.7 copy-start.3
  126.2 0.7 copy-start.4
